TPU v7x, 32 devices: a whole 2x2x4 slice. The times are simulated.
32 devices in a mesh: section: 4 (over y, core), seq: 8 (over z, x).
Axes of the slice: x: 2, y: 2, z: 4, core: 2. Of those that a mesh axis runs over, the one named last changes fastest.
Arguments:
- stream: bfloat16 [4, 512, 1024], P('section', 'seq'), may hold values from -1.5 to 1.5
- queries: bfloat16 [4, 512, 1024], P('section', 'seq'), may hold values from -8 to 8
- key_rows: bfloat16 [4, 512, 1024], P('section', 'seq'), may hold values from -8 to 8
- values: bfloat16 [4, 512, 1024], P('section', 'seq'), may hold values from -36 to 36
- incoming: bfloat16 [512, 1024], P('seq'), may hold values from -1.5 to 1.5
Outputs:
- updated: bfloat16 [4, 512, 1024], P('section', 'seq')
- received: bfloat16 [4, 512, 1024], P('section', 'seq')
All inputs are finite; a program needn't handle non-finite values.
Results may differ from a plain program's by a relative error of at most 0.0054.
Values may be sent and summed in bfloat16 or wider, within the bound.
A program may use at most 64 MiB of HBM per device.

v0:
```python
import jax
import jax.numpy as jnp
from jax import lax
from jax.sharding import PartitionSpec as P

HEAD_SIZE = 128


def passed_along(value, axis, steps):
    count = lax.axis_size(axis)
    leading, last = (max(0, -steps), min(count, count - steps))
    return lax.ppermute(value, axis, [(source, source + steps) for source in range(leading, last)])


def by_heads(block_in):
    tok_count = block_in.shape[1]
    return block_in[0].reshape(tok_count, block_in.shape[2] // HEAD_SIZE, HEAD_SIZE)


def attend(query_rows, key_rows, value_rows, seq_len):
    row_count = query_rows.shape[0]
    head_count = query_rows.shape[1]
    feat_count = query_rows.shape[2]
    scale = feat_count ** (-0.5)
    seq_count = row_count // seq_len
    query_seq = query_rows.reshape(seq_count, seq_len, head_count, feat_count)
    key_seq = key_rows.reshape(seq_count, seq_len, head_count, feat_count)
    value_seq = value_rows.reshape(seq_count, seq_len, head_count, feat_count)

    def one_sequence(pieces):
        query_block, key_block, value_block = pieces
        scores = (
            jnp.einsum("qhd,khd->hqk", query_block, key_block, preferred_element_type=jnp.float32)
            * scale
        )
        highest = jnp.max(scores, axis=-1, keepdims=True)
        exponent = jnp.exp(scores - highest)
        totals = jnp.sum(exponent, axis=-1)
        weights = exponent.astype(jnp.bfloat16)
        summed = jnp.einsum(
            "hqk,khd->qhd", weights, value_block, preferred_element_type=jnp.float32
        )
        return (summed / jnp.transpose(totals)[:, :, None]).astype(jnp.bfloat16)

    output = lax.map(one_sequence, (query_seq, key_seq, value_seq))
    return output.reshape(query_rows.shape)


def per_device(stream, queries, key_rows, values, incoming):
    seq_len = 8 * queries.shape[1]
    query_heads = by_heads(queries)
    key_heads = by_heads(key_rows)
    value_heads = by_heads(values)
    query_whole = lax.all_to_all(query_heads, "seq", split_axis=1, concat_axis=0, tiled=True)
    key_whole, value_whole = (
        lax.all_to_all(key_heads, "seq", split_axis=1, concat_axis=0, tiled=True),
        lax.all_to_all(value_heads, "seq", split_axis=1, concat_axis=0, tiled=True),
    )
    result = attend(query_whole, key_whole, value_whole, seq_len)
    tokens_back = lax.all_to_all(result, "seq", split_axis=0, concat_axis=1, tiled=True).reshape(
        stream.shape
    )
    updated = (stream.astype(jnp.float32) + tokens_back.astype(jnp.float32)).astype(jnp.bfloat16)
    carried = passed_along(updated, "section", 1)
    first_section = lax.axis_index("section") == 0
    received = jnp.where(first_section, incoming[None], carried)
    return (updated, received)


def solution(mesh):
    placed = (
        P("section", "seq", None),
        P("section", "seq", None),
        P("section", "seq", None),
        P("section", "seq", None),
        P("seq", None),
    )
    return jax.shard_map(
        per_device,
        mesh=mesh,
        in_specs=placed,
        out_specs=(P("section", "seq", None), P("section", "seq", None)),
        check_vma=False,
    )
```

profile of v0, /device:TPU:1, one launch (start us, length us, event | category | flops | bytes accessed | tf_op | source)
XLA Modules:
  0.0 57.0 jit_solution(11182906149857331247)
XLA Ops:
  0.6 0.9 %copy.18 = bf16[8,8,8,128]{3,2,1,0:T(8,128)(2,1)S(1)} copy(bf16[8,8,8,128]{3,1,2,0:T(8,128)(2,1)} %bitcast.54) | data formatting | bytes 262144
  1.6 0.7 %copy.13 = bf16[64,8,128]{2,0,1:T(8,128)(2,1)} copy(bf16[64,8,128]{2,1,0:T(8,128)(2,1)S(1)} %bitcast.51) | data formatting | bytes 262144 | tf_op jit(solution)/shard_map/reshape;squeeze | solution.py:17
  2.2 6.5 %all-to-all-start = ((bf16[64,8,128]{2,0,1:T(8,128)(2,1)}), bf16[64,8,128]{2,0,1:T(8,128)(2,1)S(1)}, u32[]{:S(2)}, u32[]{:S(2)}) async-start(bf16[64,8,128]{2,0,1:T(8,128)(2,1)} %copy.13), calls=%async_computation | async-start | bytes 262144 | tf_op jit(solution)/shard_map/all_to_all | solution.py:54
  8.7 0.7 %copy.14 = bf16[64,8,128]{2,0,1:T(8,128)(2,1)} copy(bf16[64,8,128]{2,1,0:T(8,128)(2,1)S(1)} %bitcast.52) | data formatting | bytes 262144 | tf_op jit(solution)/shard_map/reshape;squeeze | solution.py:17
  9.4 5.5 %all-to-all-done = bf16[64,8,128]{2,0,1:T(8,128)(2,1)S(1)} async-done(((bf16[64,8,128]{2,0,1:T(8,128)(2,1)}), bf16[64,8,128]{2,0,1:T(8,128)(2,1)S(1)}, u32[]{:S(2)}, u32[]{:S(2)}) %all-to-all-start) | async-done | bytes 131104 | tf_op jit(solution)/shard_map/all_to_all | solution.py:54
  14.9 3.4 %all-to-all-start.1 = ((bf16[64,8,128]{2,0,1:T(8,128)(2,1)}), bf16[64,8,128]{2,0,1:T(8,128)(2,1)S(1)}, u32[]{:S(2)}, u32[]{:S(2)}) async-start(bf16[64,8,128]{2,0,1:T(8,128)(2,1)} %copy.14), calls=%async_computation.1 | async-start | bytes 262144 | tf_op jit(solution)/shard_map/all_to_all | solution.py:56
  18.3 0.7 %copy.15 = bf16[64,8,128]{2,0,1:T(8,128)(2,1)} copy(bf16[64,8,128]{2,1,0:T(8,128)(2,1)S(1)} %bitcast.53) | data formatting | bytes 262144 | tf_op jit(solution)/shard_map/reshape;squeeze | solution.py:17
  19.0 5.4 %all-to-all-done.1 = bf16[64,8,128]{2,0,1:T(8,128)(2,1)S(1)} async-done(((bf16[64,8,128]{2,0,1:T(8,128)(2,1)}), bf16[64,8,128]{2,0,1:T(8,128)(2,1)S(1)}, u32[]{:S(2)}, u32[]{:S(2)}) %all-to-all-start.1) | async-done | bytes 131104 | tf_op jit(solution)/shard_map/all_to_all | solution.py:56
  24.4 3.4 %all-to-all-start.2 = ((bf16[64,8,128]{2,0,1:T(8,128)(2,1)}), bf16[64,8,128]{2,0,1:T(8,128)(2,1)S(1)}, u32[]{:S(2)}, u32[]{:S(2)}) async-start(bf16[64,8,128]{2,0,1:T(8,128)(2,1)} %copy.15), calls=%async_computation.2 | async-start | bytes 262144 | tf_op jit(solution)/shard_map/all_to_all | solution.py:57
  27.8 0.3 fusion.7
  28.1 0.2 fusion.3
  28.3 5.6 %all-to-all-done.2 = bf16[64,8,128]{2,0,1:T(8,128)(2,1)S(1)} async-done(((bf16[64,8,128]{2,0,1:T(8,128)(2,1)}), bf16[64,8,128]{2,0,1:T(8,128)(2,1)S(1)}, u32[]{:S(2)}, u32[]{:S(2)}) %all-to-all-start.2) | async-done | bytes 131104 | tf_op jit(solution)/shard_map/all_to_all | solution.py:57
  33.9 0.4 fusion.2
  34.3 0.5 broadcast.13
  34.8 0.7 %reduce.4 = bf16[512,128]{1,0:T(8,128)(2,1)S(1)} reduce(bf16[512,1,128]{2,0,1:T(8,128)(2,1)S(1)} %fusion.2, bf16[]{:T(256)} %broadcast.13), dimensions={1}, to_apply=%copy.16.reduce_sub_computation | reduce | bytes 262146 | tf_op jit(solution)/shard_map/while/body/eval_jaxpr/convert_element_type | solution.py:43
  35.5 8.6 %all_to_all.54 = bf16[8,2,4096]{2,1,0:T(2,128)(2,1)S(1)} all-to-all(bf16[8,2,4096]{2,1,0:T(2,128)(2,1)S(1)} %reshape.68), channel_id=1, replica_groups=mesh['section'=4,'seq'=8] {'seq'}, dimensions={0} | all-to-all | bytes 262144 | tf_op jit(solution)/shard_map/all_to_all | solution.py:60
  44.1 0.1 reshape.69
  44.2 0.3 convert_element_type.49
  44.5 0.2 copy.17
  44.8 0.8 %copy-done.3 = bf16[1,64,1024]{2,1,0:T(8,128)(2,1)S(1)} copy-done((bf16[1,64,1024]{2,1,0:T(8,128)(2,1)S(1)}, bf16[1,64,1024]{2,1,0:T(8,128)(2,1)}, u32[]{:S(2)}) %copy-start.3) | copy-done | bytes 131096
  45.6 0.0 copy-start.4
  45.6 8.7 %collective-permute-start = (bf16[1,64,1024]{2,1,0:T(8,128)(2,1)S(1)}, bf16[1,64,1024]{2,1,0:T(8,128)(2,1)S(1)}, u32[]{:S(2)}, u32[]{:S(2)}) collective-permute-start(bf16[1,64,1024]{2,1,0:T(8,128)(2,1)S(1)} %add_convert_fusion), channel_id=1, source_target_pairs={{0,8},{8,16},{16,24},{1,9},{9,17},{17,25},{2,10},{10,18},{18,26},{... | collective-permute-start | bytes 393224 | tf_op jit(solution)/shard_map/ppermute | solution.py:12
  54.4 1.9 %collective-permute-done = bf16[1,64,1024]{2,1,0:T(8,128)(2,1)S(1)} collective-permute-done((bf16[1,64,1024]{2,1,0:T(8,128)(2,1)S(1)}, bf16[1,64,1024]{2,1,0:T(8,128)(2,1)S(1)}, u32[]{:S(2)}, u32[]{:S(2)}) %collective-permute-start) | collective-permute-done | bytes 131104 | tf_op jit(solution)/shard_map/ppermute | solution.py:12
  56.3 0.7 %bitcast_select_fusion = bf16[1,64,1024]{2,1,0:T(8,128)(2,1)} fusion(bf16[1,64,1024]{2,1,0:T(8,128)(2,1)S(1)} %collective-permute-done, bf16[64,1024]{1,0:T(8,128)(2,1)S(1)} %copy-done.2, pred[]{:T(512)S(6)} %eq.3), kind=kLoop, calls=%fused_computation.10 | loop fusion | flops 65536 | bytes 393217 | tf_op jit(solution)/shard_map/jit(_where)/select_n | solution.py:66
  (13 shorter events, 0.2 us)
Async XLA Ops:
  2.2 6.5 %copy-start = (bf16[1,64,1024]{2,1,0:T(8,128)(2,1)S(1)}, bf16[1,64,1024]{2,1,0:T(8,128)(2,1)}, u32[]{:S(2)}) copy-start(bf16[1,64,1024]{2,1,0:T(8,128)(2,1)} %param.7) | copy-start | bytes 393220
  2.2 12.7 %all-to-all-start = ((bf16[64,8,128]{2,0,1:T(8,128)(2,1)}), bf16[64,8,128]{2,0,1:T(8,128)(2,1)S(1)}, u32[]{:S(2)}, u32[]{:S(2)}) async-start(bf16[64,8,128]{2,0,1:T(8,128)(2,1)} %copy.13), calls=%async_computation | async-start | bytes 262144 | tf_op jit(solution)/shard_map/all_to_all | solution.py:54
  9.4 8.9 %copy-start.1 = (bf16[1,64,1024]{2,1,0:T(8,128)(2,1)S(1)}, bf16[1,64,1024]{2,1,0:T(8,128)(2,1)}, u32[]{:S(2)}) copy-start(bf16[1,64,1024]{2,1,0:T(8,128)(2,1)} %param.8) | copy-start | bytes 393220
  14.9 9.5 %all-to-all-start.1 = ((bf16[64,8,128]{2,0,1:T(8,128)(2,1)}), bf16[64,8,128]{2,0,1:T(8,128)(2,1)S(1)}, u32[]{:S(2)}, u32[]{:S(2)}) async-start(bf16[64,8,128]{2,0,1:T(8,128)(2,1)} %copy.14), calls=%async_computation.1 | async-start | bytes 262144 | tf_op jit(solution)/shard_map/all_to_all | solution.py:56
  24.4 9.5 %all-to-all-start.2 = ((bf16[64,8,128]{2,0,1:T(8,128)(2,1)}), bf16[64,8,128]{2,0,1:T(8,128)(2,1)S(1)}, u32[]{:S(2)}, u32[]{:S(2)}) async-start(bf16[64,8,128]{2,0,1:T(8,128)(2,1)} %copy.15), calls=%async_computation.2 | async-start | bytes 262144 | tf_op jit(solution)/shard_map/all_to_all | solution.py:57
  44.7 0.9 %copy-start.3 = (bf16[1,64,1024]{2,1,0:T(8,128)(2,1)S(1)}, bf16[1,64,1024]{2,1,0:T(8,128)(2,1)}, u32[]{:S(2)}) copy-start(bf16[1,64,1024]{2,1,0:T(8,128)(2,1)} %param.5) | copy-start | bytes 393220
  45.6 10.7 %copy-start.2 = (bf16[64,1024]{1,0:T(8,128)(2,1)S(1)}, bf16[64,1024]{1,0:T(8,128)(2,1)}, u32[]{:S(2)}) copy-start(bf16[64,1024]{1,0:T(8,128)(2,1)} %param.9) | copy-start | bytes 393220
  45.6 11.3 %copy-start.4 = (bf16[1,64,1024]{2,1,0:T(8,128)(2,1)}, bf16[1,64,1024]{2,1,0:T(8,128)(2,1)S(1)}, u32[]{:S(2)}) copy-start(bf16[1,64,1024]{2,1,0:T(8,128)(2,1)S(1)} %add_convert_fusion) | copy-start | bytes 393220
  45.6 10.6 %collective-permute-start = (bf16[1,64,1024]{2,1,0:T(8,128)(2,1)S(1)}, bf16[1,64,1024]{2,1,0:T(8,128)(2,1)S(1)}, u32[]{:S(2)}, u32[]{:S(2)}) collective-permute-start(bf16[1,64,1024]{2,1,0:T(8,128)(2,1)S(1)} %add_convert_fusion), channel_id=1, source_target_pairs={{0,8},{8,16},{16,24},{1,9},{9,17},{17,25},{2,10},{10,18},{18,26},{... | collective-permute-start | bytes 393224 | tf_op jit(solution)/shard_map/ppermute | solution.py:12
where the time goes:
time: 57.5 us; the launch traced here: 57 us
  starting transfers between devices  21.9 us (38%)
  waiting for transfers between devices  18.4 us (32%)
  blocking collectives  8.59 us (15%)
  local copies, waits for them, and re-layouts  4.74 us (8%)
  other arithmetic  1.84 us (3%)
  between operations  0.76 us (1%)
  matrix products  0.67 us (1%)
    ppermute x1, starting transfers between devices, passed_along(): lax.ppermute(value, axis, [(source, source + steps) for source in range(l...  8.71 us
    all_to_all x1, blocking collectives, per_device(): lax.all_to_all(result, 'seq', split_axis=0, concat_axis=1, tiled=True)  8.59 us
    all_to_all x1, starting transfers between devices, per_device(): lax.all_to_all(query_heads, 'seq', split_axis=1, concat_axis=0, tiled=True)  6.47 us
    all_to_all x1, waiting for transfers between devices, per_device(): lax.all_to_all(value_heads, 'seq', split_axis=1, concat_axis=0, tiled=True)  5.62 us
    all_to_all x1, waiting for transfers between devices, per_device(): lax.all_to_all(query_heads, 'seq', split_axis=1, concat_axis=0, tiled=True)  5.48 us
    all_to_all x1, waiting for transfers between devices, per_device(): lax.all_to_all(key_heads, 'seq', split_axis=1, concat_axis=0, tiled=True)  5.43 us
    all_to_all x1, starting transfers between devices, per_device(): lax.all_to_all(key_heads, 'seq', split_axis=1, concat_axis=0, tiled=True)  3.37 us
    all_to_all x1, starting transfers between devices, per_device(): lax.all_to_all(value_heads, 'seq', split_axis=1, concat_axis=0, tiled=True)  3.37 us
  transfers between devices with their start and end apart: 4, of which 4 were waited for; matrix products, arithmetic and copies ran while one was open for 3% of the time, Pallas kernels for 0%

commit v1 on v0

v1 whole, which is shorter than its diff:
```python
import functools

import jax
import jax.numpy as jnp
from jax import lax
from jax.experimental import pallas as pl
from jax.experimental.pallas import tpu as pltpu
from jax.sharding import PartitionSpec as P

HEAD_SIZE = 128
GROUP = 8
LOG2_E = 1.4426950408889634
MESH = pl.DeviceIdType.MESH


def flipped(place, mask):
    result, weight = 0, 1
    while weight < GROUP:
        bit = lax.rem(lax.div(place, weight), 2)
        result = result + weight * ((1 - bit) if mask & weight else bit)
        weight *= 2
    return result


def kernel(
    sections,
    stream_hbm, query_hbm, key_hbm, value_hbm, incoming_hbm,
    updated_ref, received_ref,
    stream_own, query_own, key_own, value_own,
    query_all, key_all, value_all, result, attended,
    load_sem, own_sem, send_sem, recv_sem, back_send, back_recv, pass_send, pass_recv, first_sem,
):
    section = lax.axis_index("section")
    seq = lax.axis_index("seq")
    me = lax.rem(seq, GROUP)
    base = seq - me
    width = query_all.shape[2]
    masks = list(range(GROUP - 1, 0, -1))
    place = {mask: flipped(me, mask) for mask in range(GROUP)}

    def columns(mask):
        return pl.ds(pl.multiple_of(place[mask] * width, HEAD_SIZE), width)

    sources = (key_hbm, value_hbm, query_hbm)
    held = (key_own, value_own, query_own)
    whole = (key_all, value_all, query_all)
    loads = [pltpu.make_async_copy(sources[i], held[i], load_sem.at[i]) for i in range(3)]
    loads.append(pltpu.make_async_copy(stream_hbm, stream_own, load_sem.at[3]))
    owns = [
        pltpu.make_async_copy(sources[i].at[:, columns(0)], whole[i].at[0], own_sem.at[i])
        for i in range(3)
    ]
    loads[0].start()
    loads[1].start()
    loads[2].start()

    barrier = pltpu.get_barrier_semaphore()
    for mask in masks:
        pl.semaphore_signal(
            barrier, inc=1, device_id={"seq": base + place[mask]}, device_id_type=MESH
        )
    previous = lax.rem(section + sections - 1, sections)
    pl.semaphore_signal(barrier, inc=1, device_id={"section": previous}, device_id_type=MESH)
    for own in owns:
        own.start()
    loads[3].start()
    first = pltpu.make_async_copy(incoming_hbm, received_ref, first_sem)

    @pl.when(section == 0)
    def _():
        first.start()

    def exchange(kind, mask):
        return pltpu.make_async_remote_copy(
            src_ref=held[kind].at[:, columns(mask)],
            dst_ref=whole[kind].at[mask],
            send_sem=send_sem.at[kind, mask],
            recv_sem=recv_sem.at[kind, mask],
            device_id={"seq": base + place[mask]},
            device_id_type=MESH,
        )

    def giving_back(mask):
        return pltpu.make_async_remote_copy(
            src_ref=result.at[mask],
            dst_ref=attended.at[mask],
            send_sem=back_send.at[mask],
            recv_sem=back_recv.at[mask],
            device_id={"seq": base + place[mask]},
            device_id_type=MESH,
        )

    def passing(mask):
        return pltpu.make_async_remote_copy(
            src_ref=updated_ref.at[:, columns(mask)],
            dst_ref=received_ref.at[:, columns(mask)],
            send_sem=pass_send.at[mask],
            recv_sem=pass_recv.at[mask],
            device_id={"section": lax.rem(section + 1, sections)},
            device_id_type=MESH,
        )

    pl.semaphore_wait(barrier, GROUP)
    for kind in range(3):
        loads[kind].wait()
        for mask in masks:
            exchange(kind, mask).start()
    for own in owns:
        own.wait()
    loads[3].wait()
    for kind in range(2):
        for mask in masks:
            exchange(kind, mask).wait_recv()

    factor = HEAD_SIZE ** -0.5 * LOG2_E

    def attend(mask):
        for start in range(0, width, HEAD_SIZE):
            feats = pl.ds(start, HEAD_SIZE)
            keys = key_all[:, :, feats].reshape(-1, HEAD_SIZE)
            vals = value_all[:, :, feats].reshape(-1, HEAD_SIZE)
            scores = lax.dot_general(
                query_all[mask, :, feats], keys, (((1,), (1,)), ((), ())),
                preferred_element_type=jnp.float32,
            )
            highest = jnp.max(scores, axis=-1, keepdims=True)
            exponent = jnp.exp2((scores - highest) * factor)
            totals = jnp.sum(exponent, axis=-1, keepdims=True)
            summed = jnp.dot(
                exponent.astype(jnp.bfloat16), vals, preferred_element_type=jnp.float32
            )
            result[mask, :, feats] = (summed / totals).astype(jnp.bfloat16)

    def update(mask, piece):
        cols = columns(mask)
        updated_ref[:, cols] = (
            stream_own[:, cols].astype(jnp.float32) + piece.astype(jnp.float32)
        ).astype(jnp.bfloat16)

        @pl.when(section < sections - 1)
        def _():
            passing(mask).start()

    attend(0)
    update(0, result[0])
    for mask in masks:
        exchange(2, mask).wait_recv()
        attend(mask)
        giving_back(mask).start()
    for mask in masks:
        giving_back(mask).wait_recv()
        update(mask, attended[mask])

    for mask in masks:
        for kind in range(3):
            exchange(kind, mask).wait_send()
        giving_back(mask).wait_send()

    @pl.when(section < sections - 1)
    def _():
        for mask in range(GROUP):
            passing(mask).wait_send()

    @pl.when(section > 0)
    def _():
        for mask in range(GROUP):
            passing(mask).wait_recv()

    @pl.when(section == 0)
    def _():
        first.wait()


def per_device(sections, stream, queries, key_rows, values, incoming):
    rows, features = incoming.shape
    width = features // GROUP
    block = jax.ShapeDtypeStruct((rows, features), jnp.bfloat16)
    own = pltpu.VMEM((rows, features), jnp.bfloat16)
    whole = pltpu.VMEM((GROUP, rows, width), jnp.bfloat16)
    updated, received = pl.pallas_call(
        functools.partial(kernel, sections),
        out_shape=(block, block),
        in_specs=[pl.BlockSpec(memory_space=pl.ANY)] * 5,
        out_specs=(pl.BlockSpec(memory_space=pltpu.VMEM),) * 2,
        scratch_shapes=[own] * 4 + [whole] * 5 + [
            pltpu.SemaphoreType.DMA((4,)),
            pltpu.SemaphoreType.DMA((3,)),
            pltpu.SemaphoreType.DMA((3, GROUP)),
            pltpu.SemaphoreType.DMA((3, GROUP)),
            pltpu.SemaphoreType.DMA((GROUP,)),
            pltpu.SemaphoreType.DMA((GROUP,)),
            pltpu.SemaphoreType.DMA((GROUP,)),
            pltpu.SemaphoreType.DMA((GROUP,)),
            pltpu.SemaphoreType.DMA,
        ],
        compiler_params=pltpu.CompilerParams(collective_id=0, has_side_effects=True),
    )(stream[0], queries[0], key_rows[0], values[0], incoming)
    return updated[None], received[None]


def solution(mesh):
    placed = (
        P("section", "seq", None),
        P("section", "seq", None),
        P("section", "seq", None),
        P("section", "seq", None),
        P("seq", None),
    )
    return jax.shard_map(
        functools.partial(per_device, mesh.shape["section"]),
        mesh=mesh,
        in_specs=placed,
        out_specs=(P("section", "seq", None), P("section", "seq", None)),
        check_vma=False,
    )
```

time: 57.5 us -> 26.2 us (0.46)
  Pallas kernels: 0 us -> 23 us
  starting transfers between devices: 21.9 us -> 0 us
  waiting for transfers between devices: 18.4 us -> 0 us
  blocking collectives: 8.59 us -> 0 us
  local copies, waits for them, and re-layouts: 4.74 us -> 2.26 us
  other arithmetic: 1.84 us -> 0 us
  matrix products: 0.67 us -> 0 us
    pallas_call x0 -> x1, Pallas kernels: none -> 23 us  [per_device(): pl.pallas_call(functools.partial(kernel, sections), out_shape=(block, blo...]
    all_to_all x3 -> x0, waiting for transfers between devices: 16.5 us -> none  [the longest x1 5.62 us: per_device(): lax.all_to_all(value_heads, 'seq', split_axis=1, concat_axis=0, tiled=True)]
    all_to_all x3 -> x0, starting transfers between devices: 13.2 us -> none  [the longest x1 6.47 us: per_device(): lax.all_to_all(query_heads, 'seq', split_axis=1, concat_axis=0, tiled=True)]
    ppermute x1 -> x0, starting transfers between devices: 8.71 us -> none  [passed_along(): lax.ppermute(value, axis, [(source, source + steps) for source in range(l...]
    all_to_all x1 -> x0, blocking collectives: 8.59 us -> none  [per_device(): lax.all_to_all(result, 'seq', split_axis=0, concat_axis=1, tiled=True)]
    another operation x3 -> x0, local copies, waits for them, and re-layouts: 2.03 us -> none  [by_heads(): block_in[0].reshape(tok_count, block_in.shape[2] // HEAD_SIZE, HEAD_SIZE)]
    ppermute x1 -> x0, waiting for transfers between devices: 1.92 us -> none  [passed_along(): lax.ppermute(value, axis, [(source, source + steps) for source in range(l...]
    convert_element_type x3 -> x0, other arithmetic: 0.97 us -> none  [the longest x1 0.67 us: one_sequence(): return (summed / jnp.transpose(totals)[:, :, None]).astype(jnp.bfloat16)]
  transfers between devices with their start and end apart: 4 -> 0, of which waited for: 4 -> 0; matrix products, arithmetic and copies ran while one was open for 3% -> 0% of each run, Pallas kernels for 0% -> 0%
where the time goes in v1:
time: 26.2 us; the launch traced here: 26 us
  Pallas kernels  23 us (88%)
  local copies, waits for them, and re-layouts  2.26 us (9%)
  between operations  0.65 us (2%)
    pallas_call x1, Pallas kernels, per_device(): pl.pallas_call(functools.partial(kernel, sections), out_shape=(block, blo...  23 us
    unnamed x4, local copies, waits for them, and re-layouts  2.26 us

profile of v1, /device:TPU:1, one launch (start us, length us, event | category | flops | bytes accessed | tf_op | source)
XLA Modules:
  0.0 26.0 jit_solution(10392765950906548322)
XLA Ops:
  0.6 23.0 %shard_map.68 = (bf16[64,1024]{1,0:T(8,128)(2,1)}, bf16[64,1024]{1,0:T(8,128)(2,1)}) custom-call(bf16[64,1024]{1,0:T(8,128)(2,1)} %bitcast.6, bf16[64,1024]{1,0:T(8,128)(2,1)} %bitcast.7, bf16[64,1024]{1,0:T(8,128)(2,1)} %bitcast.8, bf16[64,1024]{1,0:T(8,128)(2,1)} %bitcast.9, bf16[64,1024]{1,0:T(8,128)(2,1)} %incoming_hbm.1), custom_call_target="tpu_custom_call" | custom-call | tf_op jit(solution)/shard_map/pallas_call | solution.py:180
  23.7 0.0 copy-start
  23.7 1.6 %copy.9 = bf16[1,64,1024]{2,1,0:T(8,128)(2,1)} copy(bf16[1,64,1024]{2,1,0:T(8,128)(2,1)} %bitcast.11) | data formatting | bytes 262144
  25.3 0.0 copy-done
  25.3 0.7 %copy.10 = bf16[1,64,1024]{2,1,0:T(8,128)(2,1)} copy(bf16[1,64,1024]{2,1,0:T(8,128)(2,1)S(1)} %bitcast.10) | data formatting | bytes 262144
Async XLA Ops:
  23.7 1.6 %copy-start = (bf16[64,1024]{1,0:T(8,128)(2,1)S(1)}, bf16[64,1024]{1,0:T(8,128)(2,1)}, u32[]{:S(2)}) copy-start(bf16[64,1024]{1,0:T(8,128)(2,1)} %get-tuple-element.5) | copy-start | bytes 393220

commit v2 on v1

--- a/solution.py
+++ b/solution.py
@@ -25,11 +25,12 @@
 def kernel(
     sections,
     stream_hbm, query_hbm, key_hbm, value_hbm, incoming_hbm,
-    updated_ref, received_ref,
+    both_ref,
     stream_own, query_own, key_own, value_own,
     query_all, key_all, value_all, result, attended,
     load_sem, own_sem, send_sem, recv_sem, back_send, back_recv, pass_send, pass_recv, first_sem,
 ):
+    updated_ref, received_ref = both_ref.at[0], both_ref.at[1]
     section = lax.axis_index("section")
     seq = lax.axis_index("seq")
     me = lax.rem(seq, GROUP)
@@ -174,14 +175,14 @@
 def per_device(sections, stream, queries, key_rows, values, incoming):
     rows, features = incoming.shape
     width = features // GROUP
-    block = jax.ShapeDtypeStruct((rows, features), jnp.bfloat16)
+    block = pltpu.VMEM((2, rows, features), jnp.bfloat16)
     own = pltpu.VMEM((rows, features), jnp.bfloat16)
     whole = pltpu.VMEM((GROUP, rows, width), jnp.bfloat16)
-    updated, received = pl.pallas_call(
+    both = pl.pallas_call(
         functools.partial(kernel, sections),
-        out_shape=(block, block),
+        out_shape=block,
         in_specs=[pl.BlockSpec(memory_space=pl.ANY)] * 5,
-        out_specs=(pl.BlockSpec(memory_space=pltpu.VMEM),) * 2,
+        out_specs=pl.BlockSpec(memory_space=pltpu.VMEM),
         scratch_shapes=[own] * 4 + [whole] * 5 + [
             pltpu.SemaphoreType.DMA((4,)),
             pltpu.SemaphoreType.DMA((3,)),
@@ -195,7 +196,7 @@
         ],
         compiler_params=pltpu.CompilerParams(collective_id=0, has_side_effects=True),
     )(stream[0], queries[0], key_rows[0], values[0], incoming)
-    return updated[None], received[None]
+    return both[:1], both[1:]
 
 
 def solution(mesh):

time: 26.2 us -> 24 us (0.916)
  local copies, waits for them, and re-layouts: 2.26 us -> 0.72 us
  Pallas kernels: 23 us -> 22.4 us
    unnamed x4 -> x0, local copies, waits for them, and re-layouts: 2.26 us -> none
    slice x0 -> x1, local copies, waits for them, and re-layouts: none -> 0.72 us  [per_device(): return (both[:1], both[1:])]
    pallas_call x1, Pallas kernels: 23 us -> 22.4 us  [per_device(): pl.pallas_call(functools.partial(kernel, sections), out_shape=block, in_s...]
where the time goes in v2:
time: 24 us; the launch traced here: 23.7 us
  Pallas kernels  22.4 us (93%)
  local copies, waits for them, and re-layouts  0.72 us (3%)
  between operations  0.64 us (3%)
    pallas_call x1, Pallas kernels, per_device(): pl.pallas_call(functools.partial(kernel, sections), out_shape=block, in_s...  22.4 us
    slice x1, local copies, waits for them, and re-layouts, per_device(): return (both[:1], both[1:])  0.72 us

profile of v2, /device:TPU:1, one launch (start us, length us, event | category | flops | bytes accessed | tf_op | source)
XLA Modules:
  0.0 23.7 jit_solution(17286634828707306729)
XLA Ops:
  0.6 22.4 %shard_map.68 = bf16[2,64,1024]{2,1,0:T(8,128)(2,1)S(1)} custom-call(bf16[64,1024]{1,0:T(8,128)(2,1)} %bitcast.4, bf16[64,1024]{1,0:T(8,128)(2,1)} %bitcast.5, bf16[64,1024]{1,0:T(8,128)(2,1)} %bitcast.6, bf16[64,1024]{1,0:T(8,128)(2,1)} %bitcast.7, bf16[64,1024]{1,0:T(8,128)(2,1)} %incoming_hbm.1), custom_call_target="tpu_custom_call" | custom-call | tf_op jit(solution)/shard_map/pallas_call | solution.py:181
  23.0 0.7 %fusion = (bf16[1,64,1024]{2,1,0:T(8,128)(2,1)}, bf16[1,64,1024]{2,1,0:T(8,128)(2,1)}) fusion(bf16[2,64,1024]{2,1,0:T(8,128)(2,1)S(1)} %shard_map.68), kind=kLoop, calls=%fused_computation | loop fusion | bytes 524288 | tf_op jit(solution)/shard_map/slice | solution.py:199

commit v3 on v2

--- a/solution.py
+++ b/solution.py
@@ -28,7 +28,7 @@
     both_ref,
     stream_own, query_own, key_own, value_own,
     query_all, key_all, value_all, result, attended,
-    load_sem, own_sem, send_sem, recv_sem, back_send, back_recv, pass_send, pass_recv, first_sem,
+    load_sem, own_sem, send_sem, recv_sem, back_send, back_recv, pass_send, pass_recv, first_sem, known_sem,
 ):
     updated_ref, received_ref = both_ref.at[0], both_ref.at[1]
     section = lax.axis_index("section")
@@ -36,7 +36,7 @@
     me = lax.rem(seq, GROUP)
     base = seq - me
     width = query_all.shape[2]
-    masks = list(range(GROUP - 1, 0, -1))
+    masks = [6, 7, 4, 5, 3, 2, 1]
     place = {mask: flipped(me, mask) for mask in range(GROUP)}
 
     def columns(mask):
@@ -56,7 +56,7 @@
     loads[2].start()
 
     barrier = pltpu.get_barrier_semaphore()
-    for mask in masks:
+    for mask in (4, 2, 1):
         pl.semaphore_signal(
             barrier, inc=1, device_id={"seq": base + place[mask]}, device_id_type=MESH
         )
@@ -101,11 +101,31 @@
             device_id_type=MESH,
         )
 
-    pl.semaphore_wait(barrier, GROUP)
+    def tell(index, mask):
+        pl.semaphore_signal(
+            known_sem.at[index], inc=1,
+            device_id={"seq": base + place[mask]}, device_id_type=MESH,
+        )
+
+    def send(kinds, *to):
+        for mask in to:
+            for kind in kinds:
+                exchange(kind, mask).start()
+
+    pl.semaphore_wait(barrier, 4)
+    tell(0, 1)
+    tell(1, 2)
     for kind in range(3):
         loads[kind].wait()
-        for mask in masks:
-            exchange(kind, mask).start()
+    send((0, 1), 4, 1)
+    pl.semaphore_wait(known_sem.at[0], 1)
+    send((0, 1), 5)
+    pl.semaphore_wait(known_sem.at[1], 1)
+    tell(2, 1)
+    send((0, 1), 6, 2)
+    pl.semaphore_wait(known_sem.at[2], 1)
+    send((0, 1), 7, 3)
+    send((2,), *masks)
     for own in owns:
         own.wait()
     loads[3].wait()
@@ -142,12 +162,13 @@
         def _():
             passing(mask).start()
 
-    attend(0)
-    update(0, result[0])
     for mask in masks:
         exchange(2, mask).wait_recv()
         attend(mask)
         giving_back(mask).start()
+        if mask == masks[6]:
+            attend(0)
+            update(0, result[0])
     for mask in masks:
         giving_back(mask).wait_recv()
         update(mask, attended[mask])
@@ -193,6 +214,7 @@
             pltpu.SemaphoreType.DMA((GROUP,)),
             pltpu.SemaphoreType.DMA((GROUP,)),
             pltpu.SemaphoreType.DMA,
+            pltpu.SemaphoreType.REGULAR((3,)),
         ],
         compiler_params=pltpu.CompilerParams(collective_id=0, has_side_effects=True),
     )(stream[0], queries[0], key_rows[0], values[0], incoming)

time: 24 us -> 23.4 us (0.975)
  Pallas kernels: 22.4 us -> 21.8 us
    pallas_call x1, Pallas kernels: 22.4 us -> 21.8 us  [per_device(): pl.pallas_call(functools.partial(kernel, sections), out_shape=block, in_s...]
where the time goes in v3:
time: 23.4 us; the launch traced here: 23.1 us
  Pallas kernels  21.8 us (93%)
  local copies, waits for them, and re-layouts  0.72 us (3%)
  between operations  0.64 us (3%)
    pallas_call x1, Pallas kernels, per_device(): pl.pallas_call(functools.partial(kernel, sections), out_shape=block, in_s...  21.8 us
    slice x1, local copies, waits for them, and re-layouts, per_device(): return (both[:1], both[1:])  0.72 us

profile of v3, /device:TPU:1, one launch (start us, length us, event | category | flops | bytes accessed | tf_op | source)
XLA Modules:
  0.0 23.1 jit_solution(15365343529885100031)
XLA Ops:
  0.6 21.8 %shard_map.68 = bf16[2,64,1024]{2,1,0:T(8,128)(2,1)S(1)} custom-call(bf16[64,1024]{1,0:T(8,128)(2,1)} %bitcast.4, bf16[64,1024]{1,0:T(8,128)(2,1)} %bitcast.5, bf16[64,1024]{1,0:T(8,128)(2,1)} %bitcast.6, bf16[64,1024]{1,0:T(8,128)(2,1)} %bitcast.7, bf16[64,1024]{1,0:T(8,128)(2,1)} %incoming_hbm.1), custom_call_target="tpu_custom_call" | custom-call | tf_op jit(solution)/shard_map/pallas_call | solution.py:202
  22.4 0.7 %fusion = (bf16[1,64,1024]{2,1,0:T(8,128)(2,1)}, bf16[1,64,1024]{2,1,0:T(8,128)(2,1)}) fusion(bf16[2,64,1024]{2,1,0:T(8,128)(2,1)S(1)} %shard_map.68), kind=kLoop, calls=%fused_computation | loop fusion | bytes 524288 | tf_op jit(solution)/shard_map/slice | solution.py:221

commit v4 on v3

--- a/solution.py
+++ b/solution.py
@@ -36,8 +36,11 @@
     me = lax.rem(seq, GROUP)
     base = seq - me
     width = query_all.shape[2]
-    masks = [6, 7, 4, 5, 3, 2, 1]
+    masks = [1, 6, 7, 4, 5, 3, 2]
     place = {mask: flipped(me, mask) for mask in range(GROUP)}
+
+    def columns_of(partner):
+        return pl.ds(pl.multiple_of((partner - base) * width, HEAD_SIZE), width)
 
     def columns(mask):
         return pl.ds(pl.multiple_of(place[mask] * width, HEAD_SIZE), width)
@@ -71,23 +74,25 @@
     def _():
         first.start()
 
-    def exchange(kind, mask):
+    def exchange(kind, mask, partner=None):
+        partner = base + place[mask] if partner is None else partner
         return pltpu.make_async_remote_copy(
-            src_ref=held[kind].at[:, columns(mask)],
+            src_ref=held[kind].at[:, columns_of(partner)],
             dst_ref=whole[kind].at[mask],
             send_sem=send_sem.at[kind, mask],
             recv_sem=recv_sem.at[kind, mask],
-            device_id={"seq": base + place[mask]},
+            device_id={"seq": partner},
             device_id_type=MESH,
         )
 
-    def giving_back(mask):
+    def giving_back(mask, partner=None):
+        partner = base + place[mask] if partner is None else partner
         return pltpu.make_async_remote_copy(
             src_ref=result.at[mask],
             dst_ref=attended.at[mask],
             send_sem=back_send.at[mask],
             recv_sem=back_recv.at[mask],
-            device_id={"seq": base + place[mask]},
+            device_id={"seq": partner},
             device_id_type=MESH,
         )
 
@@ -122,9 +127,9 @@
     send((0, 1), 5)
     pl.semaphore_wait(known_sem.at[1], 1)
     tell(2, 1)
-    send((0, 1), 6, 2)
+    send((0, 1), 6)
     pl.semaphore_wait(known_sem.at[2], 1)
-    send((0, 1), 7, 3)
+    send((0, 1), 7, 3, 2)
     send((2,), *masks)
     for own in owns:
         own.wait()
@@ -150,7 +155,7 @@
             summed = jnp.dot(
                 exponent.astype(jnp.bfloat16), vals, preferred_element_type=jnp.float32
             )
-            result[mask, :, feats] = (summed / totals).astype(jnp.bfloat16)
+            result[mask, :, feats] = (summed * (1.0 / totals)).astype(jnp.bfloat16)
 
     def update(mask, piece):
         cols = columns(mask)
@@ -162,13 +167,23 @@
         def _():
             passing(mask).start()
 
+    def serve(mask, partner):
+        exchange(2, mask, partner).wait_recv()
+        attend(mask)
+        giving_back(mask, partner).start()
+
+    @pl.when(me > 0)
+    def _():
+        serve(me, base)
+
     for mask in masks:
-        exchange(2, mask).wait_recv()
-        attend(mask)
-        giving_back(mask).start()
-        if mask == masks[6]:
-            attend(0)
-            update(0, result[0])
+
+        @pl.when(me != mask)
+        def _():
+            serve(mask, base + place[mask])
+
+    attend(0)
+    update(0, result[0])
     for mask in masks:
         giving_back(mask).wait_recv()
         update(mask, attended[mask])

time: 23.4 us -> 22.2 us (0.949)
  the two profiles are of different devices: /device:TPU:1 before, /device:TPU:3 now
where the time goes in v4:
time: 22.2 us; the launch traced here: 22 us
  Pallas kernels  20.7 us (93%)
  local copies, waits for them, and re-layouts  0.72 us (3%)
  between operations  0.64 us (3%)
    pallas_call x1, Pallas kernels, per_device(): pl.pallas_call(functools.partial(kernel, sections), out_shape=block, in_s...  20.7 us
    slice x1, local copies, waits for them, and re-layouts, per_device(): return (both[:1], both[1:])  0.72 us

profile of v4, /device:TPU:3, one launch (start us, length us, event | category | flops | bytes accessed | tf_op | source)
XLA Modules:
  0.0 22.0 jit_solution(17558793878018599944)
XLA Ops:
  0.6 20.7 %shard_map.68 = bf16[2,64,1024]{2,1,0:T(8,128)(2,1)S(1)} custom-call(bf16[64,1024]{1,0:T(8,128)(2,1)} %bitcast.4, bf16[64,1024]{1,0:T(8,128)(2,1)} %bitcast.5, bf16[64,1024]{1,0:T(8,128)(2,1)} %bitcast.6, bf16[64,1024]{1,0:T(8,128)(2,1)} %bitcast.7, bf16[64,1024]{1,0:T(8,128)(2,1)} %incoming_hbm.1), custom_call_target="tpu_custom_call" | custom-call | tf_op jit(solution)/shard_map/pallas_call | solution.py:217
  21.3 0.7 %fusion = (bf16[1,64,1024]{2,1,0:T(8,128)(2,1)}, bf16[1,64,1024]{2,1,0:T(8,128)(2,1)}) fusion(bf16[2,64,1024]{2,1,0:T(8,128)(2,1)S(1)} %shard_map.68), kind=kLoop, calls=%fused_computation | loop fusion | bytes 524288 | tf_op jit(solution)/shard_map/slice | solution.py:236
